TPU v7x, 32 devices: a whole 2x2x4 slice. The times are simulated.
32 devices in a mesh: dp: 8 (over z, y), group: 4 (over x, core).
Axes of the slice: x: 2, y: 2, z: 4, core: 2. Of those that a mesh axis runs over, the one named last changes fastest.
Arguments:
- images: bfloat16 [1536, 768], P(('dp', 'group')), may hold values from -1.5 to 1.5, as said below
- texts: bfloat16 [1536, 768], P(('dp', 'group')), may hold values from -1.5 to 1.5
- send_pos: int32 [4, 384], P('group'), may hold values from 0 to 95, as said below
- recv_slot: int32 [32, 4, 3], P(('dp', 'group')), may hold values from 0 to 7, as said below
- counts: int32 [32, 4], P(('dp', 'group')), may hold values from 1 to 3, as said below
Outputs:
- image_grads: float32 [1536, 768], P(('dp', 'group'))
- caption_grads: float32 [256, 768], P(('dp', 'group'))
Inputs may be any that keep to these rules, and one draw needn't show every extreme that they name: `send_pos`: row g lists the pairs of group index g in order of dp index, then row. A position o * 3 + k addresses owner device o (dp index times 4 plus group index); pairs of one caption share a position; in each row every position with k < counts[o, g] is named by at least one pair, and no other position is named. `recv_slot`: the 3 entries of one owner and one sending group are different slots. `counts`: in every group index some owner receives 3 rows. `images`: rows of representations; a caption's text row and its image row are correlated.
All inputs are finite; a program needn't handle non-finite values.
Results may differ from a plain program's by a relative error of at most 0.0026.
Values may be sent and summed in bfloat16 or wider, within the bound.
A program may use at most 128 MiB of HBM per device.

v0:
```python
import jax
import jax.numpy as jnp
from jax import lax
from jax.sharding import PartitionSpec as P

CAP = 3
SLOTS = 8


LOGIT_SCALE = 14.285714


def on_device(images, texts, send_pos, recv_slot, counts):
    pair_rows = images.shape[0]
    embed_width = images.shape[1]
    group_count = lax.axis_size("group")
    data_size = lax.axis_size("dp")
    data_index = lax.axis_index("dp")
    group_index = lax.axis_index("group")
    image_block = lax.all_gather(images, "group", axis=0, tiled=True)
    text_block = lax.all_gather(texts, "dp", axis=0, tiled=True)
    logits = LOGIT_SCALE * jnp.einsum(
        "re,ce->rc", image_block, text_block, preferred_element_type=jnp.float32
    )
    row_high = jnp.max(logits, axis=1)
    column_high = jnp.max(logits, axis=0)
    row_high = lax.pmax(row_high, "group")
    column_high = lax.pmax(column_high, "dp")
    row_total = lax.psum(jnp.sum(jnp.exp(logits - row_high[:, None]), axis=1), "group")
    column_total = lax.psum(jnp.sum(jnp.exp(logits - column_high[None, :]), axis=0), "dp")
    row_norms = row_high + jnp.log(row_total)
    column_norms = column_high + jnp.log(column_total)
    row_local = jnp.arange(image_block.shape[0], dtype=jnp.int32)
    column_local = jnp.arange(text_block.shape[0], dtype=jnp.int32)
    row_pair = (
        data_index * group_count + row_local // pair_rows
    ) * pair_rows + row_local % pair_rows
    column_pair = (
        column_local // pair_rows * group_count + group_index
    ) * pair_rows + column_local % pair_rows
    diagonal = (row_pair[:, None] == column_pair[None, :]).astype(jnp.float32)
    weights = (
        0.5 * jnp.exp(logits - row_norms[:, None])
        + 0.5 * jnp.exp(logits - column_norms[None, :])
        - diagonal
    ).astype(jnp.bfloat16)
    image_part = jnp.dot(weights, text_block, preferred_element_type=jnp.float32)
    image_grads = LOGIT_SCALE * lax.psum_scatter(
        image_part, "group", scatter_dimension=0, tiled=True
    )
    position_count = data_size * group_count * CAP
    column_partial = jnp.einsum(
        "rc,re->ce", weights, image_block, preferred_element_type=jnp.float32
    )
    owner_rows = LOGIT_SCALE * jax.ops.segment_sum(
        column_partial, send_pos[0], num_segments=position_count
    )
    sectioned = owner_rows.reshape(data_size, group_count * CAP, embed_width)
    sectioned = lax.all_to_all(sectioned, "dp", split_axis=0, concat_axis=0, tiled=True)
    reduced = jnp.sum(sectioned, axis=0).reshape(group_count, CAP, embed_width)
    arrived = lax.all_to_all(reduced, "group", split_axis=0, concat_axis=0, tiled=True)
    live_rows = jnp.arange(CAP, dtype=jnp.int32)[None, :] < counts[0][:, None]
    slot_match = (
        recv_slot[0][:, :, None] == jnp.arange(SLOTS, dtype=jnp.int32)[None, None, :]
    ) & live_rows[:, :, None]
    caption_grads = jnp.einsum(
        "gks,gke->se", slot_match.astype(jnp.float32), arrived, precision=lax.Precision.HIGHEST
    )
    return (image_grads, caption_grads)


def solution(mesh):
    placed = (
        P(("dp", "group"), None),
        P(("dp", "group"), None),
        P("group", None),
        P(("dp", "group"), None, None),
        P(("dp", "group"), None),
    )
    return jax.shard_map(
        on_device,
        mesh=mesh,
        in_specs=placed,
        out_specs=(P(("dp", "group"), None), P(("dp", "group"), None)),
        check_vma=False,
    )
```

profile of v0, /device:TPU:1, one launch (start us, length us, event | category | flops | bytes accessed | tf_op | source)
XLA Modules:
  0.0 134.3 jit_solution(11347326508840474663)
XLA Ops:
  7.2 0.0 reduce-scatter.2.cloned.1.call-start
  7.2 27.3 %all_gather.7 = bf16[384,768]{1,0:T(8,128)(2,1)S(1)} all-gather(bf16[48,768]{1,0:T(8,128)(2,1)} %param.6), channel_id=1, replica_groups=mesh['dp'=8,'group'=4] {'dp'}, dimensions={0}, use_global_device_ids=true | all-gather | bytes 663552 | tf_op jit(solution)/shard_map/all_gather | solution.py:21
  34.5 12.2 %all_gather.6 = bf16[192,768]{1,0:T(8,128)(2,1)S(1)} all-gather(bf16[48,768]{1,0:T(8,128)(2,1)} %param.5), channel_id=1, replica_groups=mesh['dp'=8,'group'=4] {'group'}, dimensions={0}, use_global_device_ids=true | all-gather | bytes 368640 | tf_op jit(solution)/shard_map/all_gather | solution.py:20
  46.7 0.5 fusion.25
  47.1 17.7 %pmax.15 = f32[384]{0:T(512)S(1)} all-reduce(f32[384]{0:T(512)S(1)} %get-tuple-element.5), channel_id=1, replica_groups=mesh['dp'=8,'group'=4] {'dp'}, use_global_device_ids=true, to_apply=%region_5.0 | all-reduce | flops 384 | bytes 3072 | tf_op jit(solution)/shard_map/pmax | solution.py:28
  64.9 9.0 %pmax.14 = f32[192]{0:T(256)S(1)} all-reduce(f32[192]{0:T(256)S(1)} %get-tuple-element.4), channel_id=1, replica_groups=mesh['dp'=8,'group'=4] {'group'}, use_global_device_ids=true, to_apply=%region_1.0 | all-reduce | flops 192 | bytes 1536 | tf_op jit(solution)/shard_map/pmax | solution.py:27
  73.8 0.2 exponential_reduce_fusion.1
  74.0 13.7 %psum.15 = f32[384]{0:T(512)S(1)} all-reduce(f32[384]{0:T(512)S(1)} %get-tuple-element.3), channel_id=1, replica_groups=mesh['dp'=8,'group'=4] {'dp'}, use_global_device_ids=true, to_apply=%region_7.0 | all-reduce | flops 384 | bytes 3072 | tf_op jit(solution)/shard_map/psum | solution.py:30
  87.7 9.2 %psum.14 = f32[192]{0:T(256)S(1)} all-reduce(f32[192]{0:T(256)S(1)} %get-tuple-element.2), channel_id=1, replica_groups=mesh['dp'=8,'group'=4] {'group'}, use_global_device_ids=true, to_apply=%region_3.0 | all-reduce | flops 192 | bytes 1536 | tf_op jit(solution)/shard_map/psum | solution.py:29
  96.9 1.2 fusion.24
  98.1 0.0 copy-start.1
  98.1 0.0 reduce-scatter.2.cloned.1.call-update
  98.2 0.5 fusion.23
  98.7 0.2 copy-done.1
  98.8 3.1 %scatter_custom_fusion = f32[96,768]{1,0:T(8,128)S(1)} fusion(s32[384]{0:T(512)S(1)} %reduce, f32[384,768]{1,0:T(8,128)S(1)} %fusion.23, f32[]{:T(128)} %constant.26.clone.1), kind=kCustom, calls=%fused_computation.7 | custom fusion | flops 294912 | bytes 294916 | tf_op jit(solution)/shard_map/scatter-add | solution.py:55
  102.0 0.0 copy-start.2
  102.0 0.0 copy-start
  102.1 13.3 %all_to_all.10 = f32[8,12,768]{2,1,0:T(8,128)S(1)} all-to-all(f32[8,12,768]{2,1,0:T(8,128)S(1)} %reshape.80), channel_id=1, replica_groups=mesh['dp'=8,'group'=4] {'dp'}, dimensions={0} | all-to-all | bytes 589824 | tf_op jit(solution)/shard_map/all_to_all | solution.py:59
  115.3 0.6 reshape.81
  116.0 5.8 %all-to-all-start.1 = ((f32[4,3,768]{2,1,0:T(4,128)}), f32[4,3,768]{2,1,0:T(4,128)S(1)}, u32[]{:S(2)}, u32[]{:S(2)}) async-start(f32[4,3,768]{2,1,0:T(4,128)} %reshape.81), calls=%async_computation.2 | async-start | bytes 98304 | tf_op jit(solution)/shard_map/all_to_all | solution.py:61
  121.8 0.0 copy-done.2
  121.8 0.0 copy-done
  121.8 3.2 %all-to-all-done.1 = f32[4,3,768]{2,1,0:T(4,128)S(1)} async-done(((f32[4,3,768]{2,1,0:T(4,128)}), f32[4,3,768]{2,1,0:T(4,128)S(1)}, u32[]{:S(2)}, u32[]{:S(2)}) %all-to-all-start.1) | async-done | bytes 36896 | tf_op jit(solution)/shard_map/all_to_all | solution.py:61
  125.0 0.9 convolution_bitcast_fusion
  125.9 0.0 reduce-scatter.2.cloned.1.call-done
  125.9 1.6 %broadcast_multiply_fusion.1 = f32[48,768]{1,0:T(8,128)} fusion(f32[48,768]{1,0:T(8,128)} %reduce-scatter.2.cloned.1.call-done), kind=kLoop, calls=%fused_computation.9 | loop fusion | flops 36864 | bytes 294912 | tf_op jit(solution)/shard_map/mul | solution.py:48
  (10 shorter events, 0.2 us)
Async XLA Ops:
  7.2 118.7 %reduce-scatter.2.cloned.1.call-start = ((), (), s32[]{:S(2)}) async-start(), calls=%async_computation.3 | async-start | bytes 737280 | tf_op jit(solution)/shard_map/reduce_scatter | solution.py:48
  98.1 0.7 copy-start.1
  102.0 19.8 %copy-start.2 = (s32[1,4]{1,0:T(1,128)S(1)}, s32[1,4]{1,0:T(1,128)}, u32[]{:S(2)}) copy-start(s32[1,4]{1,0:T(1,128)} %param.9) | copy-start | bytes 52
  102.0 19.8 %copy-start = (s32[1,4,3]{1,0,2:T(1,128)S(1)}, s32[1,4,3]{1,0,2:T(1,128)}, u32[]{:S(2)}) copy-start(s32[1,4,3]{1,0,2:T(1,128)} %param.8) | copy-start | bytes 148
  116.0 9.0 %all-to-all-start.1 = ((f32[4,3,768]{2,1,0:T(4,128)}), f32[4,3,768]{2,1,0:T(4,128)S(1)}, u32[]{:S(2)}, u32[]{:S(2)}) async-start(f32[4,3,768]{2,1,0:T(4,128)} %reshape.81), calls=%async_computation.2 | async-start | bytes 98304 | tf_op jit(solution)/shard_map/all_to_all | solution.py:61
Sparse Core Ops, SparseCore 0:
  98.3 20.8 reduce-scatter.1
where the time goes:
time: 136 us; the launch traced here: 134 us
  blocking collectives  102 us (75%)
  between operations  14.1 us (10%)
  starting transfers between devices  5.83 us (4%)
  other arithmetic  5.02 us (4%)
  waiting for transfers between devices  3.2 us (2%)
  matrix products  3.06 us (2%)
    all_gather x1, blocking collectives, on_device(): text_block = lax.all_gather(texts, 'dp', axis=0, tiled=True)  27.3 us
    pmax x1, blocking collectives, on_device(): column_high = lax.pmax(column_high, 'dp')  17.7 us
    psum x1, blocking collectives, on_device(): lax.psum(jnp.sum(jnp.exp(logits - column_high[None, :]), axis=0), 'dp')  13.7 us
    all_to_all x1, blocking collectives, on_device(): lax.all_to_all(sectioned, 'dp', split_axis=0, concat_axis=0, tiled=True)  13.3 us
    all_gather x1, blocking collectives, on_device(): image_block = lax.all_gather(images, 'group', axis=0, tiled=True)  12.2 us
    psum x1, blocking collectives, on_device(): lax.psum(jnp.sum(jnp.exp(logits - row_high[:, None]), axis=1), 'group')  9.23 us
    pmax x1, blocking collectives, on_device(): row_high = lax.pmax(row_high, 'group')  8.95 us
    all_to_all x1, starting transfers between devices, on_device(): lax.all_to_all(reduced, 'group', split_axis=0, concat_axis=0, tiled=True)  5.79 us
  transfers between devices with their start and end apart: 2, of which 1 were waited for; matrix products, arithmetic and copies ran while one was open for 4% of the time, Pallas kernels for 0%

commit v1 on v0

v1 whole, which is shorter than its diff:
```python
import functools

import jax
import jax.numpy as jnp
from jax import lax
from jax.experimental import pallas as pl
from jax.experimental.pallas import tpu as pltpu
from jax.sharding import PartitionSpec as P

CAP = 3
SLOTS = 8
PAD = 4
LOGIT_SCALE = 14.285714
MESH = pl.DeviceIdType.MESH
F32 = jnp.float32
BF16 = jnp.bfloat16


def loop(count, body):
    if count <= 8:
        for step in range(count):
            body(step)
    else:
        lax.fori_loop(0, count, lambda step, _: (body(step), 0)[1], 0)


def dot_nt(left, right):
    return lax.dot_general(left, right, (((1,), (1,)), ((), ())), preferred_element_type=F32)


def dot_nn(left, right):
    return lax.dot_general(left, right, (((1,), (0,)), ((), ())), preferred_element_type=F32)


def merge_lse(parts):
    high = functools.reduce(jnp.maximum, parts)
    return high + jnp.log(functools.reduce(jnp.add, [jnp.exp(part - high) for part in parts]))


def kernel(
    dp_count, group_count, columns, images, texts, send_pos, recv_slot, counts,
    image_grads, caption_grads,
    image_all, text_all, logits, row_high, row_total, row_lse, column_lse, own_row, own_column,
    weights, part_send, part_recv, cap_send, cap_recv,
    image_send_sem, image_recv_sem, text_send_sem, text_recv_sem,
    row_send_sem, row_recv_sem, column_send_sem, column_recv_sem,
    part_send_sem, part_recv_sem, cap_send_sem, cap_recv_sem,
):
    rows = images.shape[0]
    width = images.shape[1]
    block_rows = group_count * rows
    chunk_count = dp_count * rows // columns
    device_count = dp_count * group_count
    d = lax.axis_index("dp")
    g = lax.axis_index("group")
    me = d * group_count + g
    twin = d + 1 - 2 * (d % 2)
    half = dp_count // 2

    def peer_dp(step):
        return (d + 1 + step) % dp_count

    def peer_group(step):
        return (g + 1 + step) % group_count

    def peer_same(step):
        return ((d // 2 + 1 + step) % half) * 2 + d % 2

    def wait_bytes(ref, sem):
        pltpu.make_async_copy(ref, ref, sem).wait()

    barrier = pltpu.get_barrier_semaphore()
    loop(dp_count - 1, lambda step: pl.semaphore_signal(
        barrier, inc=1, device_id=(peer_dp(step), g), device_id_type=MESH))
    loop(group_count - 1, lambda step: pl.semaphore_signal(
        barrier, inc=1, device_id=(d, peer_group(step)), device_id_type=MESH))

    own_image_rows = pl.ds(pl.multiple_of(g * rows, 16), rows)
    own_text_rows = pl.ds(pl.multiple_of(d * rows, 16), rows)
    image_all[own_image_rows, :] = images[...]
    text_all[own_text_rows, :] = texts[...]
    pl.semaphore_wait(barrier, dp_count + group_count - 2)

    def text_rows(source):
        return text_all.at[pl.ds(pl.multiple_of(source * rows, 16), rows), :]

    def text_copy(source_ref, source, target):
        return pltpu.make_async_remote_copy(
            src_ref=source_ref, dst_ref=text_rows(source),
            send_sem=text_send_sem.at[0], recv_sem=text_recv_sem.at[source],
            device_id=(target, g), device_id_type=MESH)

    loop(half - 1, lambda step: text_copy(texts, d, peer_same(step)).start())
    text_copy(texts, d, twin).start()

    def image_copy(step):
        return pltpu.make_async_remote_copy(
            src_ref=images, dst_ref=image_all.at[own_image_rows, :],
            send_sem=image_send_sem.at[0], recv_sem=image_recv_sem.at[0],
            device_id=(d, peer_group(step)), device_id_type=MESH)

    loop(group_count - 1, lambda step: image_copy(step).start())

    def arrived(source):
        text_copy(texts, source, twin).wait_recv()

    def forward(step):
        source = (d // 2 + half - 1 - step) % half * 2 + d % 2
        arrived(source)
        text_copy(text_rows(source), source, twin).start()

    loop(half - 1, forward)
    loop(half, lambda step: arrived((twin // 2 + half - step) % half * 2 + twin % 2))
    wait_bytes(image_all.at[pl.ds(0, (group_count - 1) * rows), :], image_recv_sem.at[0])

    row_high[...] = jnp.full_like(row_high, -jnp.inf)
    row_total[...] = jnp.zeros_like(row_total)

    def columns_of(chunk):
        return pl.ds(pl.multiple_of(chunk * columns, 128), columns)

    def text_chunk(chunk):
        return text_all[pl.ds(pl.multiple_of(chunk * columns, 16), columns), :]

    def logit_step(chunk):
        block = LOGIT_SCALE * dot_nt(image_all[...], text_chunk(chunk))
        logits[chunk] = block
        row_high[...] = jnp.maximum(row_high[...], jnp.max(block, axis=1, keepdims=True))
        high = jnp.max(block, axis=0, keepdims=True)
        own_column[:, columns_of(chunk)] = high + jnp.log(
            jnp.sum(jnp.exp(block - high), axis=0, keepdims=True))

    loop(chunk_count, logit_step)

    def column_copy(step):
        return pltpu.make_async_remote_copy(
            src_ref=own_column, dst_ref=column_lse.at[d],
            send_sem=column_send_sem.at[0], recv_sem=column_recv_sem.at[0],
            device_id=(peer_dp(step), g), device_id_type=MESH)

    loop(dp_count - 1, lambda step: column_copy(step).start())
    column_lse[d] = own_column[...]

    def total_step(chunk):
        row_total[...] += jnp.sum(jnp.exp(logits[chunk] - row_high[...]), axis=1, keepdims=True)

    loop(chunk_count, total_step)
    diagonal = (
        lax.broadcasted_iota(jnp.int32, (block_rows, block_rows), 0)
        == lax.broadcasted_iota(jnp.int32, (block_rows, block_rows), 1)
    )
    lse = row_high[...] + jnp.log(row_total[...])
    own_row[...] = jnp.sum(jnp.where(diagonal, lse, 0.0), axis=0, keepdims=True)

    def row_copy(step):
        return pltpu.make_async_remote_copy(
            src_ref=own_row, dst_ref=row_lse.at[g],
            send_sem=row_send_sem.at[0], recv_sem=row_recv_sem.at[0],
            device_id=(d, peer_group(step)), device_id_type=MESH)

    loop(group_count - 1, lambda step: row_copy(step).start())
    row_lse[g] = own_row[...]
    wait_bytes(row_lse.at[pl.ds(0, group_count - 1)], row_recv_sem.at[0])
    row_norm = merge_lse([row_lse[source] for source in range(group_count)])
    row_norm = jnp.sum(jnp.where(diagonal, row_norm, 0.0), axis=1, keepdims=True)
    row_high[...] = row_norm
    wait_bytes(column_lse.at[pl.ds(0, dp_count - 1)], column_recv_sem.at[0])

    def weight_step(chunk):
        where = columns_of(chunk)
        column_norm = merge_lse([column_lse[source, :, where] for source in range(dp_count)])
        block = logits[chunk]
        row = lax.broadcasted_iota(jnp.int32, block.shape, 0) - g * rows
        column = lax.broadcasted_iota(jnp.int32, block.shape, 1) + (chunk * columns - d * rows)
        same = (row == column) & (row >= 0) & (row < rows)
        weights[chunk] = (
            0.5 * jnp.exp(block - row_high[...])
            + 0.5 * jnp.exp(block - column_norm)
            - same.astype(F32)
        ).astype(BF16)

    loop(chunk_count, weight_step)

    owner_block = 32
    merged_rows = owner_block * PAD

    def caption_step(step):
        index = lax.broadcasted_iota(jnp.int32, (merged_rows, columns), 0)
        within = index % PAD
        position = jnp.where(
            within < CAP, (step * owner_block + index // PAD) * CAP + within, -1)
        merged = jnp.zeros((merged_rows, block_rows), F32)
        if chunk_count == 1:
            chosen = (send_pos[...] == position).astype(BF16)
            merged = dot_nt(chosen, weights[0])
        else:
            def add(chunk, total):
                chosen = (send_pos[:, columns_of(chunk)] == position).astype(BF16)
                return total + dot_nt(chosen, weights[chunk])
            merged = lax.fori_loop(0, chunk_count, add, merged)
        coarse = merged.astype(BF16)
        fine = (merged - coarse.astype(F32)).astype(BF16)
        block = LOGIT_SCALE * (dot_nn(coarse, image_all[...]) + dot_nn(fine, image_all[...]))
        cap_send[pl.ds(step * owner_block, owner_block)] = block.reshape(
            owner_block, PAD, width).astype(BF16)

    loop(device_count // owner_block, caption_step)

    def cap_copy(step):
        target = (me + 1 + step) % device_count
        return pltpu.make_async_remote_copy(
            src_ref=cap_send.at[target], dst_ref=cap_recv.at[me],
            send_sem=cap_send_sem.at[0], recv_sem=cap_recv_sem.at[0],
            device_id=(target // group_count, target % group_count), device_id_type=MESH)

    lax.fori_loop(0, device_count - 1, lambda step, _: (cap_copy(step).start(), 0)[1], 0)
    cap_recv[me] = cap_send[me]

    if chunk_count == 1:
        part = dot_nn(weights[0], text_chunk(0))
    else:
        part = lax.fori_loop(
            0, chunk_count,
            lambda chunk, total: total + dot_nn(weights[chunk], text_chunk(chunk)),
            jnp.zeros((block_rows, width), F32))
    part = LOGIT_SCALE * part
    for target in range(group_count):
        part_send[target] = part[target * rows:(target + 1) * rows].astype(BF16)

    def part_copy(step):
        target = peer_group(step)
        return pltpu.make_async_remote_copy(
            src_ref=part_send.at[target], dst_ref=part_recv.at[g],
            send_sem=part_send_sem.at[0], recv_sem=part_recv_sem.at[0],
            device_id=(d, target), device_id_type=MESH)

    loop(group_count - 1, lambda step: part_copy(step).start())
    part_recv[g] = part_send[g]
    wait_bytes(part_recv.at[pl.ds(0, group_count - 1)], part_recv_sem.at[0])
    image_grads[...] = functools.reduce(
        jnp.add, [part_recv[source].astype(F32) for source in range(group_count)])

    wait_bytes(cap_recv.at[pl.ds(0, device_count - 1)], cap_recv_sem.at[0])
    slot = lax.broadcasted_iota(jnp.int32, (SLOTS, width), 0)
    result = jnp.zeros((SLOTS, width), F32)
    for source in range(group_count):
        if dp_count <= 8:
            total = functools.reduce(
                jnp.add,
                [cap_recv[q * group_count + source].astype(F32) for q in range(dp_count)])
        else:
            total = lax.fori_loop(
                0, dp_count,
                lambda q, total: total + cap_recv[q * group_count + source].astype(F32),
                jnp.zeros((PAD, width), F32))
        for k in range(CAP):
            live = k < counts[0, source]
            chosen = jnp.where(live, recv_slot[0, source, k], SLOTS)
            result = result + jnp.where(slot == chosen, total[k:k + 1], 0.0)
    caption_grads[...] = result

    wait_bytes(text_all.at[pl.ds(0, (dp_count - 1) * rows), :], text_send_sem.at[0])
    wait_bytes(image_all.at[pl.ds(0, (group_count - 1) * rows), :], image_send_sem.at[0])
    wait_bytes(column_lse.at[pl.ds(0, dp_count - 1)], column_send_sem.at[0])
    wait_bytes(row_lse.at[pl.ds(0, group_count - 1)], row_send_sem.at[0])
    wait_bytes(part_recv.at[pl.ds(0, group_count - 1)], part_send_sem.at[0])
    wait_bytes(cap_recv.at[pl.ds(0, device_count - 1)], cap_send_sem.at[0])


def on_device(dp_count, group_count, images, texts, send_pos, recv_slot, counts):
    rows, width = images.shape
    block_rows = group_count * rows
    total = dp_count * rows
    columns = min(dp_count, 8) * rows
    chunks = total // columns
    devices = dp_count * group_count
    vmem = pl.BlockSpec(memory_space=pltpu.VMEM)
    smem = pl.BlockSpec(memory_space=pltpu.SMEM)
    dma = pltpu.SemaphoreType.DMA
    return pl.pallas_call(
        functools.partial(kernel, dp_count, group_count, columns),
        out_shape=(
            jax.ShapeDtypeStruct((rows, width), F32),
            jax.ShapeDtypeStruct((SLOTS, width), F32),
        ),
        in_specs=[vmem, vmem, vmem, smem, smem],
        out_specs=(vmem, vmem),
        scratch_shapes=[
            pltpu.VMEM((block_rows, width), BF16),
            pltpu.VMEM((total, width), BF16),
            pltpu.VMEM((chunks, block_rows, columns), F32),
            pltpu.VMEM((block_rows, 1), F32),
            pltpu.VMEM((block_rows, 1), F32),
            pltpu.VMEM((group_count, 1, block_rows), F32),
            pltpu.VMEM((dp_count, 1, total), F32),
            pltpu.VMEM((1, block_rows), F32),
            pltpu.VMEM((1, total), F32),
            pltpu.VMEM((chunks, block_rows, columns), BF16),
            pltpu.VMEM((group_count, rows, width), BF16),
            pltpu.VMEM((group_count, rows, width), BF16),
            pltpu.VMEM((devices, PAD, width), BF16),
            pltpu.VMEM((devices, PAD, width), BF16),
            dma((1,)), dma((1,)), dma((1,)), dma((dp_count,)),
            dma((1,)), dma((1,)), dma((1,)), dma((1,)),
            dma((1,)), dma((1,)), dma((1,)), dma((1,)),
        ],
        compiler_params=pltpu.CompilerParams(
            collective_id=0, has_side_effects=True, vmem_limit_bytes=60 * 1024 * 1024),
    )(images, texts, send_pos, recv_slot, counts)


def solution(mesh):
    placed = (
        P(("dp", "group"), None),
        P(("dp", "group"), None),
        P("group", None),
        P(("dp", "group"), None, None),
        P(("dp", "group"), None),
    )
    return jax.shard_map(
        functools.partial(on_device, mesh.shape["dp"], mesh.shape["group"]),
        mesh=mesh,
        in_specs=placed,
        out_specs=(P(("dp", "group"), None), P(("dp", "group"), None)),
        check_vma=False,
    )
```

time: 136 us -> 34.6 us (0.25); the launches traced: 134 us -> 34.4 us
  blocking collectives: 102 us -> 0 us
  Pallas kernels: 0 us -> 30.2 us
  between operations: 14.1 us -> 0.65 us
  starting transfers between devices: 5.83 us -> 0 us
  other arithmetic: 5.02 us -> 0 us
  waiting for transfers between devices: 3.2 us -> 0 us
  matrix products: 3.06 us -> 0 us
  local copies, waits for them, and re-layouts: 0.85 us -> 3.54 us
    all_gather x2 -> x0, blocking collectives: 39.4 us -> none  [the longest x1 27.3 us: on_device(): text_block = lax.all_gather(texts, 'dp', axis=0, tiled=True)]
    pallas_call x0 -> x1, Pallas kernels: none -> 30.2 us  [on_device(): pl.pallas_call(functools.partial(kernel, dp_count, group_count, columns),...]
    pmax x2 -> x0, blocking collectives: 26.7 us -> none  [the longest x1 17.7 us: on_device(): column_high = lax.pmax(column_high, 'dp')]
    psum x2 -> x0, blocking collectives: 22.9 us -> none  [the longest x1 13.7 us: on_device(): lax.psum(jnp.sum(jnp.exp(logits - column_high[None, :]), axis=0), 'dp')]
    all_to_all x1 -> x0, blocking collectives: 13.3 us -> none  [on_device(): lax.all_to_all(sectioned, 'dp', split_axis=0, concat_axis=0, tiled=True)]
    all_to_all x1 -> x0, starting transfers between devices: 5.79 us -> none  [on_device(): lax.all_to_all(reduced, 'group', split_axis=0, concat_axis=0, tiled=True)]
    unnamed x6 -> x5, local copies, waits for them, and re-layouts: 0.18 us -> 3.54 us
    all_to_all x1 -> x0, waiting for transfers between devices: 3.19 us -> none  [on_device(): lax.all_to_all(reduced, 'group', split_axis=0, concat_axis=0, tiled=True)]
  transfers between devices with their start and end apart: 2 -> 0, of which waited for: 1 -> 0; matrix products, arithmetic and copies ran while one was open for 4% -> 0% of each run, Pallas kernels for 0% -> 0%
where the time goes in v1:
time: 34.6 us; the launch traced here: 34.4 us
  Pallas kernels  30.2 us (87%)
  local copies, waits for them, and re-layouts  3.54 us (10%)
  between operations  0.65 us (2%)
    pallas_call x1, Pallas kernels, on_device(): pl.pallas_call(functools.partial(kernel, dp_count, group_count, columns),...  30.2 us
    unnamed x5, local copies, waits for them, and re-layouts  3.54 us

profile of v1, /device:TPU:1, one launch (start us, length us, event | category | flops | bytes accessed | tf_op | source)
XLA Modules:
  0.0 34.4 jit_solution(14704898859975358438)
XLA Ops:
  0.6 1.3 %copy.7.recv_slot = s32[1,4,3]{2,1,0:T(4,128)} copy(s32[1,4,3]{1,0,2:T(1,128)} %param.8) | data formatting | bytes 96 | tf_op args[3]
  2.0 30.2 %shard_map.68 = (f32[48,768]{1,0:T(8,128)}, f32[8,768]{1,0:T(8,128)}) custom-call(bf16[48,768]{1,0:T(8,128)(2,1)} %images.1, bf16[48,768]{1,0:T(8,128)(2,1)} %texts.1, s32[1,384]{1,0:T(1,128)} %send_pos.1, s32[1,4,3]{2,1,0:T(4,128)} %copy.7.recv_slot, s32[1,4]{1,0:T(1,128)} %counts.1), custom_call_target="tpu_custom_call" | custom-call | tf_op jit(solution)/shard_map/pallas_call | solution.py:280
  32.2 0.0 copy-start
  32.2 1.6 %copy.10 = f32[48,768]{1,0:T(8,128)} copy(f32[48,768]{1,0:T(8,128)} %get-tuple-element.4) | data formatting | bytes 294912
  33.8 0.0 copy-done
  33.8 0.6 %copy.11 = f32[8,768]{1,0:T(8,128)} copy(f32[8,768]{1,0:T(8,128)S(1)} %copy-done) | data formatting | bytes 49152
Async XLA Ops:
  32.2 1.6 %copy-start = (f32[8,768]{1,0:T(8,128)S(1)}, f32[8,768]{1,0:T(8,128)}, u32[]{:S(2)}) copy-start(f32[8,768]{1,0:T(8,128)} %get-tuple-element.5) | copy-start | bytes 73732

commit v2 on v1

--- a/solution.py
+++ b/solution.py
@@ -38,10 +38,11 @@
 
 
 def kernel(
-    dp_count, group_count, columns, images, texts, send_pos, recv_slot, counts,
+    dp_count, group_count, columns, images_in, texts_in, send_pos_in, recv_slot_in, counts_in,
     image_grads, caption_grads,
+    images, texts, send_pos, recv_slot, counts, load_sem,
     image_all, text_all, logits, row_high, row_total, row_lse, column_lse, own_row, own_column,
-    weights, part_send, part_recv, cap_send, cap_recv,
+    weights, part_own, part_send, part_recv, cap_send, cap_recv,
     image_send_sem, image_recv_sem, text_send_sem, text_recv_sem,
     row_send_sem, row_recv_sem, column_send_sem, column_recv_sem,
     part_send_sem, part_recv_sem, cap_send_sem, cap_recv_sem,
@@ -75,6 +76,16 @@
     loop(group_count - 1, lambda step: pl.semaphore_signal(
         barrier, inc=1, device_id=(d, peer_group(step)), device_id_type=MESH))
 
+    loads = [
+        pltpu.make_async_copy(source, target, load_sem.at[index])
+        for index, (source, target) in enumerate((
+            (texts_in, texts), (images_in, images), (send_pos_in, send_pos),
+            (recv_slot_in, recv_slot), (counts_in, counts)))
+    ]
+    for load in loads:
+        load.start()
+    for load in loads:
+        load.wait()
     own_image_rows = pl.ds(pl.multiple_of(g * rows, 16), rows)
     own_text_rows = pl.ds(pl.multiple_of(d * rows, 16), rows)
     image_all[own_image_rows, :] = images[...]
@@ -224,6 +235,7 @@
             lambda chunk, total: total + dot_nn(weights[chunk], text_chunk(chunk)),
             jnp.zeros((block_rows, width), F32))
     part = LOGIT_SCALE * part
+    part_own[...] = part
     for target in range(group_count):
         part_send[target] = part[target * rows:(target + 1) * rows].astype(BF16)
 
@@ -235,9 +247,9 @@
             device_id=(d, target), device_id_type=MESH)
 
     loop(group_count - 1, lambda step: part_copy(step).start())
-    part_recv[g] = part_send[g]
+    part_recv[g] = jnp.zeros((rows, width), BF16)
     wait_bytes(part_recv.at[pl.ds(0, group_count - 1)], part_recv_sem.at[0])
-    image_grads[...] = functools.reduce(
+    image_grads[...] = part_own[own_image_rows, :] + functools.reduce(
         jnp.add, [part_recv[source].astype(F32) for source in range(group_count)])
 
     wait_bytes(cap_recv.at[pl.ds(0, device_count - 1)], cap_recv_sem.at[0])
@@ -255,7 +267,7 @@
                 jnp.zeros((PAD, width), F32))
         for k in range(CAP):
             live = k < counts[0, source]
-            chosen = jnp.where(live, recv_slot[0, source, k], SLOTS)
+            chosen = jnp.where(live, recv_slot[k, 0, source], SLOTS)
             result = result + jnp.where(slot == chosen, total[k:k + 1], 0.0)
     caption_grads[...] = result
 
@@ -275,17 +287,23 @@
     chunks = total // columns
     devices = dp_count * group_count
     vmem = pl.BlockSpec(memory_space=pltpu.VMEM)
-    smem = pl.BlockSpec(memory_space=pltpu.SMEM)
+    anywhere = pl.BlockSpec(memory_space=pl.ANY)
     dma = pltpu.SemaphoreType.DMA
     return pl.pallas_call(
         functools.partial(kernel, dp_count, group_count, columns),
         out_shape=(
-            jax.ShapeDtypeStruct((rows, width), F32),
-            jax.ShapeDtypeStruct((SLOTS, width), F32),
+            pltpu.VMEM((rows, width), F32),
+            pltpu.VMEM((SLOTS, width), F32),
         ),
-        in_specs=[vmem, vmem, vmem, smem, smem],
+        in_specs=[anywhere] * 5,
         out_specs=(vmem, vmem),
         scratch_shapes=[
+            pltpu.VMEM((rows, width), BF16),
+            pltpu.VMEM((rows, width), BF16),
+            pltpu.VMEM((1, total), jnp.int32),
+            pltpu.SMEM((CAP, 1, group_count), jnp.int32),
+            pltpu.SMEM((1, group_count), jnp.int32),
+            dma((5,)),
             pltpu.VMEM((block_rows, width), BF16),
             pltpu.VMEM((total, width), BF16),
             pltpu.VMEM((chunks, block_rows, columns), F32),
@@ -296,6 +314,7 @@
             pltpu.VMEM((1, block_rows), F32),
             pltpu.VMEM((1, total), F32),
             pltpu.VMEM((chunks, block_rows, columns), BF16),
+            pltpu.VMEM((block_rows, width), F32),
             pltpu.VMEM((group_count, rows, width), BF16),
             pltpu.VMEM((group_count, rows, width), BF16),
             pltpu.VMEM((devices, PAD, width), BF16),
@@ -306,7 +325,7 @@
         ],
         compiler_params=pltpu.CompilerParams(
             collective_id=0, has_side_effects=True, vmem_limit_bytes=60 * 1024 * 1024),
-    )(images, texts, send_pos, recv_slot, counts)
+    )(images, texts, send_pos, jnp.transpose(recv_slot, (2, 0, 1)), counts)
 
 
 def solution(mesh):

time: 34.6 us -> 30.7 us (0.89)
  local copies, waits for them, and re-layouts: 3.54 us -> 1.27 us
  Pallas kernels: 30.2 us -> 28.7 us
    unnamed x5 -> x2, local copies, waits for them, and re-layouts: 3.54 us -> 1.27 us
    pallas_call x1, Pallas kernels: 30.2 us -> 28.7 us  [on_device(): pl.pallas_call(functools.partial(kernel, dp_count, group_count, columns),...]
where the time goes in v2:
time: 30.7 us; the launch traced here: 30.6 us
  Pallas kernels  28.7 us (93%)
  local copies, waits for them, and re-layouts  1.27 us (4%)
  between operations  0.64 us (2%)
    pallas_call x1, Pallas kernels, on_device(): pl.pallas_call(functools.partial(kernel, dp_count, group_count, columns),...  28.7 us
    unnamed x2, local copies, waits for them, and re-layouts  1.27 us

profile of v2, /device:TPU:1, one launch (start us, length us, event | category | flops | bytes accessed | tf_op | source)
XLA Modules:
  0.0 30.6 jit_solution(13886108229124934386)
XLA Ops:
  0.6 28.7 %shard_map.68 = (f32[48,768]{1,0:T(8,128)S(1)}, f32[8,768]{1,0:T(8,128)S(1)}) custom-call(bf16[48,768]{1,0:T(8,128)(2,1)} %images_in.1, bf16[48,768]{1,0:T(8,128)(2,1)} %texts_in.1, s32[1,384]{1,0:T(1,128)} %send_pos_in.1, s32[3,1,4]{2,1,0:T(1,128)} %bitcast.1, s32[1,4]{1,0:T(1,128)} %counts_in.1), custom_call_target="tpu_custom_call" | custom-call | tf_op jit(solution)/shard_map/pallas_call | solution.py:292
  29.3 0.7 %copy.9 = f32[48,768]{1,0:T(8,128)} copy(f32[48,768]{1,0:T(8,128)S(1)} %get-tuple-element.2) | data formatting | bytes 294912
  30.0 0.6 %copy.10 = f32[8,768]{1,0:T(8,128)} copy(f32[8,768]{1,0:T(8,128)S(1)} %get-tuple-element.3) | data formatting | bytes 49152
